TPU v7x, 256 devices: a whole 4x4x8 slice. The times are simulated.
256 devices in a mesh: row: 8 (over y, z_hi), col: 32 (over x, z_lo, core).
Axes of the slice: x: 4, y: 4, z: 8 (z_hi: 2, z_lo: 4; z = z_hi * 4 + z_lo), core: 2. Of those that a mesh axis runs over, the one named last changes fastest.
Arguments:
- previous: bfloat16 [4, 128, 256, 256], P(None, 'row', 'col'), may hold values from -6 to 6
- skip_coarse: bfloat16 [4, 128, 256, 256], P(None, 'row', 'col'), may hold values from -6 to 6
- skip_fine: bfloat16 [4, 256, 512, 256], P(None, 'row', 'col'), may hold values from -6 to 6
- coarse_convs: bfloat16 [4, 3, 3, 256, 256], replicated, may hold values from -0.125 to 0.125
- coarse_biases: float32 [4, 256], replicated, may hold values from -3 to 3
- coarse_project: bfloat16 [256, 256], replicated, may hold values from -0.375 to 0.375
- coarse_offset: float32 [256], replicated, may hold values from -3 to 3
- fine_convs: bfloat16 [4, 3, 3, 256, 256], replicated, may hold values from -0.125 to 0.125
- fine_biases: float32 [4, 256], replicated, may hold values from -3 to 3
- fine_project: bfloat16 [256, 256], replicated, may hold values from -0.375 to 0.375
- fine_offset: float32 [256], replicated, may hold values from -3 to 3
Outputs:
- decoded: bfloat16 [4, 512, 1024, 256], P(None, 'row', 'col')
All inputs are finite; a program needn't handle non-finite values.
Results may differ from a plain program's by a relative error of at most 0.012.
Values may be sent and summed in bfloat16 or wider, within the bound.
A program may use at most 128 MiB of HBM per device.

v0:
```python
import jax
import jax.numpy as jnp
from jax import lax
from jax.sharding import PartitionSpec as P


def extended(cells, sides, width):
    for axis, dim in sides:
        count = lax.axis_size(axis)
        ends = count - 1
        head = lax.slice_in_dim(cells, 0, width, axis=dim)
        tail = lax.slice_in_dim(cells, cells.shape[dim] - width, cells.shape[dim], axis=dim)
        cells = jnp.concatenate(
            [
                lax.ppermute(tail, axis, [(i, (i + 1) % count) for i in range(ends)]),
                cells,
                lax.ppermute(head, axis, [((i + 1) % count, i) for i in range(ends)]),
            ],
            axis=dim,
        )
    return cells


def valid_conv(padded, kernel, bias):
    result = lax.conv_general_dilated(
        padded,
        kernel,
        (1, 1),
        "VALID",
        dimension_numbers=("NHWC", "HWIO", "NHWC"),
        preferred_element_type=jnp.float32,
    )
    return result + bias


def coarse_double(values):
    return extended(values, (("row", 1), ("col", 2)), 2)


def fine_double(values):
    return extended(values, (("row", 1), ("col", 2)), 2)


def coarse_rim(values):
    return extended(values, (("row", 1), ("col", 2)), 1)


def fine_rim(values):
    return extended(values, (("row", 1), ("col", 2)), 1)


def unit_double(inputs, kernels, biases, first, widen):
    rows = inputs.shape[1]
    cols = inputs.shape[2]
    row_place = lax.axis_index("row") * rows - 1 + jnp.arange(rows + 2)
    col_place = lax.axis_index("col") * cols - 1 + jnp.arange(cols + 2)
    row_inside = (row_place >= 0) & (row_place < rows * lax.axis_size("row"))
    col_inside = (col_place >= 0) & (col_place < cols * lax.axis_size("col"))
    inside = row_inside[None, :, None, None] & col_inside[None, None, :, None]
    active = jax.nn.relu(inputs).astype(jnp.bfloat16)
    hidden = jax.nn.relu(valid_conv(widen(active), kernels[first], biases[first]))
    hidden = jnp.where(inside, hidden, 0.0).astype(jnp.bfloat16)
    return inputs.astype(jnp.float32) + valid_conv(hidden, kernels[first + 1], biases[first + 1])


def double_inner(padded, axis):
    count = padded.shape[axis] - 2
    values = lax.slice_in_dim(padded, 1, count + 1, axis=axis)
    before = lax.slice_in_dim(padded, 0, count, axis=axis)
    after = lax.slice_in_dim(padded, 2, count + 2, axis=axis)
    stacked = jnp.stack(
        [0.75 * values + 0.25 * before, 0.75 * values + 0.25 * after], axis=axis + 1
    )
    shape = list(values.shape)
    shape[axis] = 2 * count
    return stacked.reshape(shape)


def upsample_tile(image, widen):
    padded = widen(image)
    row_id = lax.axis_index("row")
    col_id = lax.axis_index("col")
    top = jnp.where(row_id == 0, padded[:, 1:2], padded[:, 0:1])
    bottom = jnp.where(row_id == lax.axis_size("row") - 1, padded[:, -2:-1], padded[:, -1:])
    padded = jnp.concatenate([top, padded[:, 1:-1], bottom], axis=1)
    left = jnp.where(col_id == 0, padded[:, :, 1:2], padded[:, :, 0:1])
    right = jnp.where(col_id == lax.axis_size("col") - 1, padded[:, :, -2:-1], padded[:, :, -1:])
    padded = jnp.concatenate([left, padded[:, :, 1:-1], right], axis=2).astype(jnp.float32)
    rowwise = double_inner(padded, 1)
    return double_inner(rowwise, 2).astype(jnp.bfloat16)


def per_device(
    previous,
    skip_coarse,
    skip_fine,
    coarse_convs,
    coarse_biases,
    coarse_project,
    coarse_offset,
    fine_convs,
    fine_biases,
    fine_project,
    fine_offset,
):
    sum_coarse = previous.astype(jnp.float32) + unit_double(
        skip_coarse, coarse_convs, coarse_biases, 0, coarse_double
    )
    top_coarse = unit_double(sum_coarse, coarse_convs, coarse_biases, 2, coarse_double).astype(
        jnp.bfloat16
    )
    lifted = upsample_tile(top_coarse, coarse_rim)
    joined_coarse = (
        jnp.dot(lifted, coarse_project, preferred_element_type=jnp.float32) + coarse_offset
    ).astype(jnp.bfloat16)
    sum_fine = joined_coarse.astype(jnp.float32) + unit_double(
        skip_fine, fine_convs, fine_biases, 0, fine_double
    )
    top_fine = unit_double(sum_fine, fine_convs, fine_biases, 2, fine_double).astype(jnp.bfloat16)
    raised = upsample_tile(top_fine, fine_rim)
    return (jnp.dot(raised, fine_project, preferred_element_type=jnp.float32) + fine_offset).astype(
        jnp.bfloat16
    )


def solution(mesh):
    in_specs = (
        P(None, "row", "col", None),
        P(None, "row", "col", None),
        P(None, "row", "col", None),
        P(),
        P(),
        P(),
        P(),
        P(),
        P(),
        P(),
        P(),
    )
    out_specs = P(None, "row", "col", None)
    return jax.shard_map(
        per_device, mesh=mesh, in_specs=in_specs, out_specs=out_specs, check_vma=False
    )
```

profile of v0, /device:TPU:233, one launch (start us, length us, event | category | flops | bytes accessed | tf_op | source)
XLA Modules:
  0.0 253.3 jit_solution(11718758478547954897)
XLA Ops:
  1.3 4.1 %collective-permute-start = (bf16[4,2,8,256]{3,0,2,1:T(4,128)(2,1)S(1)}, bf16[4,2,8,256]{3,0,2,1:T(4,128)(2,1)S(1)}, u32[]{:S(2)}, u32[]{:S(2)}) collective-permute-start(bf16[4,2,8,256]{3,0,2,1:T(4,128)(2,1)S(1)} %get-tuple-element.39), channel_id=1, source_target_pairs={{0,32},{32,64},{64,96},{96,128},{128,160},{160,192},{192,224},{1,3... | collective-permute-start | bytes 98312 | tf_op jit(solution)/shard_map/ppermute | solution.py:15
  5.4 5.1 %collective-permute-start.1 = (bf16[4,2,8,256]{3,0,2,1:T(4,128)(2,1)S(1)}, bf16[4,2,8,256]{3,0,2,1:T(4,128)(2,1)S(1)}, u32[]{:S(2)}, u32[]{:S(2)}) collective-permute-start(bf16[4,2,8,256]{3,0,2,1:T(4,128)(2,1)S(1)} %get-tuple-element.40), channel_id=1, source_target_pairs={{32,0},{64,32},{96,64},{128,96},{160,128},{192,160},{224,192},{33,... | collective-permute-start | bytes 98312 | tf_op jit(solution)/shard_map/ppermute | solution.py:17
  12.2 5.0 %collective-permute-start.12 = (bf16[4,2,16,256]{3,1,2,0:T(2,128)(2,1)S(1)}, bf16[4,2,16,256]{3,1,2,0:T(2,128)(2,1)S(1)}, u32[]{:S(2)}, u32[]{:S(2)}) collective-permute-start(bf16[4,2,16,256]{3,1,2,0:T(2,128)(2,1)S(1)} %get-tuple-element.23), channel_id=1, source_target_pairs={{0,32},{32,64},{64,96},{96,128},{128,160},{160,192},{192,224},{1,3... | collective-permute-start | bytes 196616 | tf_op jit(solution)/shard_map/ppermute | solution.py:15
  17.2 4.2 %collective-permute-start.13 = (bf16[4,2,16,256]{3,1,2,0:T(2,128)(2,1)S(1)}, bf16[4,2,16,256]{3,1,2,0:T(2,128)(2,1)S(1)}, u32[]{:S(2)}, u32[]{:S(2)}) collective-permute-start(bf16[4,2,16,256]{3,1,2,0:T(2,128)(2,1)S(1)} %get-tuple-element.24), channel_id=1, source_target_pairs={{32,0},{64,32},{96,64},{128,96},{160,128},{192,160},{224,192},{33,... | collective-permute-start | bytes 196616 | tf_op jit(solution)/shard_map/ppermute | solution.py:17
  22.3 6.1 %collective-permute-start.2 = (bf16[4,20,2,256]{3,0,2,1:T(4,128)(2,1)S(1)}, bf16[4,20,2,256]{3,0,2,1:T(4,128)(2,1)S(1)}, u32[]{:S(2)}, u32[]{:S(2)}) collective-permute-start(bf16[4,20,2,256]{3,0,2,1:T(4,128)(2,1)S(1)} %get-tuple-element.31), channel_id=1, source_target_pairs={{0,1},{1,2},{2,3},{3,4},{4,5},{5,6},{6,7},{7,8},{8,9},{9,10},{10,1... | collective-permute-start | bytes 245768 | tf_op jit(solution)/shard_map/ppermute | solution.py:15
  28.4 1.9 collective-permute-start.3
  30.5 6.3 %collective-permute-start.14 = (bf16[4,36,2,256]{3,1,2,0:T(8,128)(2,1)S(1)}, bf16[4,36,2,256]{3,1,2,0:T(8,128)(2,1)S(1)}, u32[]{:S(2)}, u32[]{:S(2)}) collective-permute-start(bf16[4,36,2,256]{3,1,2,0:T(8,128)(2,1)S(1)} %get-tuple-element.15), channel_id=1, source_target_pairs={{0,1},{1,2},{2,3},{3,4},{4,5},{5,6},{6,7},{7,8},{8,9},{9,10},{10,1... | collective-permute-start | bytes 442376 | tf_op jit(solution)/shard_map/ppermute | solution.py:15
  36.9 1.9 collective-permute-start.15
  38.8 5.6 %maximum_convert_fusion.2 = (bf16[4,16,8,256]{3,0,2,1:T(4,128)(2,1)S(1)}, f32[4,16,8,256]{3,0,2,1:T(4,128)}) fusion(f32[256]{0:T(256)S(1)} %bitcast.138, bf16[4,3,3,256,256]{4,3,2,1,0:T(8,128)(2,1)} %param.14, bf16[4,20,2,256]{3,0,2,1:T(4,128)(2,1)S(1)} %collective-permute-done.3, bf16[4,2,8,256]{3,0,2,1:T(4,128)(2,1)S(1)} %collective-permute-done.1, ...), kind=kOutput, calls=%fused_computation.109 | convolution fusion | flops 1457438720 | bytes 4163764 | tf_op jit(solution)/shard_map/conv_general_dilated | solution.py:25
  44.5 3.6 %collective-permute-start.4 = (bf16[4,2,8,256]{3,0,2,1:T(4,128)(2,1)S(1)}, bf16[4,2,8,256]{3,0,2,1:T(4,128)(2,1)S(1)}, u32[]{:S(2)}, u32[]{:S(2)}) collective-permute-start(bf16[4,2,8,256]{3,0,2,1:T(4,128)(2,1)S(1)} %get-tuple-element.37), channel_id=1, source_target_pairs={{0,32},{32,64},{64,96},{96,128},{128,160},{160,192},{192,224},{1,3... | collective-permute-start | bytes 98312 | tf_op jit(solution)/shard_map/ppermute | solution.py:15
  48.0 5.6 %collective-permute-start.5 = (bf16[4,2,8,256]{3,0,2,1:T(4,128)(2,1)S(1)}, bf16[4,2,8,256]{3,0,2,1:T(4,128)(2,1)S(1)}, u32[]{:S(2)}, u32[]{:S(2)}) collective-permute-start(bf16[4,2,8,256]{3,0,2,1:T(4,128)(2,1)S(1)} %get-tuple-element.38), channel_id=1, source_target_pairs={{32,0},{64,32},{96,64},{128,96},{160,128},{192,160},{224,192},{33,... | collective-permute-start | bytes 98312 | tf_op jit(solution)/shard_map/ppermute | solution.py:17
  53.7 4.1 %collective-permute-done.5 = bf16[4,2,8,256]{3,0,2,1:T(4,128)(2,1)S(1)} collective-permute-done((bf16[4,2,8,256]{3,0,2,1:T(4,128)(2,1)S(1)}, bf16[4,2,8,256]{3,0,2,1:T(4,128)(2,1)S(1)}, u32[]{:S(2)}, u32[]{:S(2)}) %collective-permute-start.5) | collective-permute-done | bytes 32800 | tf_op jit(solution)/shard_map/ppermute | solution.py:17
  58.0 7.4 %collective-permute-start.6 = (bf16[4,20,2,256]{3,0,2,1:T(4,128)(2,1)S(1)}, bf16[4,20,2,256]{3,0,2,1:T(4,128)(2,1)S(1)}, u32[]{:S(2)}, u32[]{:S(2)}) collective-permute-start(bf16[4,20,2,256]{3,0,2,1:T(4,128)(2,1)S(1)} %get-tuple-element.29), channel_id=1, source_target_pairs={{0,1},{1,2},{2,3},{3,4},{4,5},{5,6},{6,7},{7,8},{8,9},{9,10},{10,1... | collective-permute-start | bytes 245768 | tf_op jit(solution)/shard_map/ppermute | solution.py:15
  65.4 1.9 collective-permute-start.7
  70.7 1.8 fusion.12
  72.5 5.4 %add_maximum_fusion.1 = bf16[34,32,3,256]{3,1,2,0:T(8,128)(2,1)S(1)} fusion(f32[256]{0:T(256)S(1)} %bitcast.137, pred[32,3]{0,1:T(4,128)(4,1)S(1)} %copy-done.11, bf16[36,4,8,5,256]{4,1,3,2,0:T(4,128)(2,1)S(1)} %fusion.12, bf16[4,3,3,256,256]{4,3,2,1,0:T(8,128)(2,1)} %param.18), kind=kOutput, calls=%fused_computation.17 | convolution fusion | flops 3853713408 | bytes 5801056 | tf_op jit(solution)/shard_map/conv_general_dilated | solution.py:25
  81.7 4.7 %fusion.46 = bf16[4,16,8,256]{3,0,2,1:T(4,128)(2,1)S(1)} fusion(f32[4,16,8,256]{3,0,2,1:T(4,128)} %get-tuple-element.50, bf16[4,3,3,256,256]{4,3,2,1,0:T(8,128)(2,1)} %param.14, bf16[4,20,2,256]{3,0,2,1:T(4,128)(2,1)} %copy-done.9, bf16[4,2,8,256]{3,0,2,1:T(4,128)(2,1)S(1)} %collective-permute-done.5, bf16[4,16,8,256]{3,0,2,1:T(4,128)(2,1)S(1)} %get-tuple-element.49, ...), kind=kOutput, calls=%fused_computation.67 | convolution fusion | flops 1456914432 | bytes 3639476 | tf_op jit(solution)/shard_map/conv_general_dilated | solution.py:25
  86.4 5.8 %collective-permute-start.8 = (bf16[4,1,8,256]{3,0,2,1:T(4,128)(2,1)S(1)}, bf16[4,1,8,256]{3,0,2,1:T(4,128)(2,1)S(1)}, u32[]{:S(2)}, u32[]{:S(2)}) collective-permute-start(bf16[4,1,8,256]{3,0,2,1:T(4,128)(2,1)S(1)} %get-tuple-element.35), channel_id=1, source_target_pairs={{0,32},{32,64},{64,96},{96,128},{128,160},{160,192},{192,224},{1,3... | collective-permute-start | bytes 49160 | tf_op jit(solution)/shard_map/ppermute | solution.py:15
  92.2 3.4 %collective-permute-start.9 = (bf16[4,1,8,256]{3,0,2,1:T(4,128)(2,1)S(1)}, bf16[4,1,8,256]{3,0,2,1:T(4,128)(2,1)S(1)}, u32[]{:S(2)}, u32[]{:S(2)}) collective-permute-start(bf16[4,1,8,256]{3,0,2,1:T(4,128)(2,1)S(1)} %get-tuple-element.36), channel_id=1, source_target_pairs={{32,0},{64,32},{96,64},{128,96},{160,128},{192,160},{224,192},{33,... | collective-permute-start | bytes 49160 | tf_op jit(solution)/shard_map/ppermute | solution.py:17
  95.6 1.6 fusion.22
  97.3 4.2 %collective-permute-done.9 = bf16[4,1,8,256]{3,0,2,1:T(4,128)(2,1)S(1)} collective-permute-done((bf16[4,1,8,256]{3,0,2,1:T(4,128)(2,1)S(1)}, bf16[4,1,8,256]{3,0,2,1:T(4,128)(2,1)S(1)}, u32[]{:S(2)}, u32[]{:S(2)}) %collective-permute-start.9) | collective-permute-done | bytes 16416 | tf_op jit(solution)/shard_map/ppermute | solution.py:17
  101.6 7.8 %collective-permute-start.10 = (bf16[4,18,1,256]{3,0,2,1:T(4,128)(2,1)S(1)}, bf16[4,18,1,256]{3,0,2,1:T(4,128)(2,1)S(1)}, u32[]{:S(2)}, u32[]{:S(2)}) collective-permute-start(bf16[4,18,1,256]{3,0,2,1:T(4,128)(2,1)S(1)} %get-tuple-element.33), channel_id=1, source_target_pairs={{0,1},{1,2},{2,3},{3,4},{4,5},{5,6},{6,7},{7,8},{8,9},{9,10},{10,1... | collective-permute-start | bytes 110600 | tf_op jit(solution)/shard_map/ppermute | solution.py:15
  109.3 13.7 %collective-permute-start.11 = (bf16[4,18,1,256]{3,0,2,1:T(4,128)(2,1)S(1)}, bf16[4,18,1,256]{3,0,2,1:T(4,128)(2,1)S(1)}, u32[]{:S(2)}, u32[]{:S(2)}) collective-permute-start(bf16[4,18,1,256]{3,0,2,1:T(4,128)(2,1)S(1)} %get-tuple-element.34), channel_id=1, source_target_pairs={{1,0},{2,1},{3,2},{4,3},{5,4},{6,5},{7,6},{8,7},{9,8},{10,9},{11,1... | collective-permute-start | bytes 110600 | tf_op jit(solution)/shard_map/ppermute | solution.py:17
  123.0 5.4 %select_add_fusion.1 = f32[32,32,3,256]{3,1,2,0:T(8,128)S(1)} fusion(f32[256]{0:T(256)S(1)} %bitcast.134, pred[32,3]{0,1:T(4,128)(4,1)S(1)} %copy-done.10, bf16[34,4,8,5,256]{4,1,3,2,0:T(4,128)(2,1)S(1)} %fusion.22, bf16[4,3,3,256,256]{4,3,2,1,0:T(8,128)(2,1)} %param.18), kind=kOutput, calls=%fused_computation.26 | convolution fusion | flops 3625451520 | bytes 7111776 | tf_op jit(solution)/shard_map/conv_general_dilated | solution.py:25
  128.4 1.8 copy.58
  136.4 3.0 %maximum_convert_fusion = (bf16[4,32,16,256]{3,2,1,0:T(8,128)(2,1)S(1)}, f32[4,32,16,256]{3,2,1,0:T(8,128)S(1)}) fusion(f32[32,4,16,256]{3,0,2,1:T(8,128)S(1)} %slice.315, bf16[4,32,16,256]{3,2,1,0:T(8,128)(2,1)} %param.13, f32[256]{0:T(256)S(1)} %copy-done.6, bf16[4,32,16,256]{3,2,1,0:T(8,128)(2,1)} %convert_element_type.63, bf16[256,256]{1,0:T(8,128)(2,1)S(1)} %copy-done.2), kind=kOutput, calls=%fused_computation.53 | convolution fusion | flops 272629760 | bytes 7472128 | tf_op jit(solution)/shard_map/dot_general | solution.py:114
  139.4 3.4 %collective-permute-start.16 = (bf16[4,2,16,256]{3,2,1,0:T(8,128)(2,1)S(1)}, bf16[4,2,16,256]{3,2,1,0:T(8,128)(2,1)S(1)}, u32[]{:S(2)}, u32[]{:S(2)}) collective-permute-start(bf16[4,2,16,256]{3,2,1,0:T(8,128)(2,1)S(1)} %get-tuple-element.21), channel_id=1, source_target_pairs={{0,32},{32,64},{64,96},{96,128},{128,160},{160,192},{192,224},{1,3... | collective-permute-start | bytes 196616 | tf_op jit(solution)/shard_map/ppermute | solution.py:15
  142.9 5.7 %collective-permute-start.17 = (bf16[4,2,16,256]{3,2,1,0:T(8,128)(2,1)S(1)}, bf16[4,2,16,256]{3,2,1,0:T(8,128)(2,1)S(1)}, u32[]{:S(2)}, u32[]{:S(2)}) collective-permute-start(bf16[4,2,16,256]{3,2,1,0:T(8,128)(2,1)S(1)} %get-tuple-element.22), channel_id=1, source_target_pairs={{32,0},{64,32},{96,64},{128,96},{160,128},{192,160},{224,192},{33,... | collective-permute-start | bytes 196616 | tf_op jit(solution)/shard_map/ppermute | solution.py:17
  148.6 4.1 %collective-permute-done.17 = bf16[4,2,16,256]{3,2,1,0:T(8,128)(2,1)S(1)} collective-permute-done((bf16[4,2,16,256]{3,2,1,0:T(8,128)(2,1)S(1)}, bf16[4,2,16,256]{3,2,1,0:T(8,128)(2,1)S(1)}, u32[]{:S(2)}, u32[]{:S(2)}) %collective-permute-start.17) | collective-permute-done | bytes 65568 | tf_op jit(solution)/shard_map/ppermute | solution.py:17
  152.9 7.8 %collective-permute-start.18 = (bf16[4,36,2,256]{3,2,1,0:T(2,128)(2,1)S(1)}, bf16[4,36,2,256]{3,2,1,0:T(2,128)(2,1)S(1)}, u32[]{:S(2)}, u32[]{:S(2)}) collective-permute-start(bf16[4,36,2,256]{3,2,1,0:T(2,128)(2,1)S(1)} %get-tuple-element.13), channel_id=1, source_target_pairs={{0,1},{1,2},{2,3},{3,4},{4,5},{5,6},{6,7},{7,8},{8,9},{9,10},{10,1... | collective-permute-start | bytes 442376 | tf_op jit(solution)/shard_map/ppermute | solution.py:15
  160.7 1.9 collective-permute-start.19
  162.8 7.1 %collective-permute-done.19 = bf16[4,36,2,256]{3,2,1,0:T(2,128)(2,1)S(1)} collective-permute-done((bf16[4,36,2,256]{3,2,1,0:T(2,128)(2,1)S(1)}, bf16[4,36,2,256]{3,2,1,0:T(2,128)(2,1)S(1)}, u32[]{:S(2)}, u32[]{:S(2)}) %collective-permute-start.19) | collective-permute-done | bytes 147488 | tf_op jit(solution)/shard_map/ppermute | solution.py:17
  173.6 1.9 fusion.13
  175.5 4.1 %add_maximum_fusion = bf16[34,32,3,256]{3,1,2,0:T(8,128)(2,1)S(1)} fusion(f32[256]{0:T(256)S(1)} %bitcast.133, pred[32,3]{0,1:T(4,128)(4,1)S(1)} %copy-done.12, bf16[36,4,8,5,256]{4,1,3,2,0:T(4,128)(2,1)S(1)} %fusion.13, bf16[4,3,3,256,256]{4,3,2,1,0:T(8,128)(2,1)S(1)} %bitcast.141), kind=kOutput, calls=%fused_computation.16 | convolution fusion | flops 3853713408 | bytes 5801472 | tf_op jit(solution)/shard_map/conv_general_dilated | solution.py:25
  184.4 4.3 %select_add_fusion = f32[32,32,3,256]{3,1,2,0:T(8,128)S(1)} fusion(f32[256]{0:T(256)S(1)} %bitcast.132, pred[32,3]{0,1:T(4,128)(4,1)S(1)} %copy-done.10, bf16[34,4,8,5,256]{4,1,3,2,0:T(4,128)(2,1)S(1)} %fusion.23, bf16[4,3,3,256,256]{4,3,2,1,0:T(8,128)(2,1)S(1)} %bitcast.141), kind=kOutput, calls=%fused_computation.25 | convolution fusion | flops 3625451520 | bytes 7112192 | tf_op jit(solution)/shard_map/conv_general_dilated | solution.py:25
  188.7 1.8 copy.65
  192.4 6.2 %collective-permute-start.20 = (bf16[4,1,16,256]{3,2,1,0:T(8,128)(2,1)S(1)}, bf16[4,1,16,256]{3,2,1,0:T(8,128)(2,1)S(1)}, u32[]{:S(2)}, u32[]{:S(2)}) collective-permute-start(bf16[4,1,16,256]{3,2,1,0:T(8,128)(2,1)S(1)} %get-tuple-element.19), channel_id=1, source_target_pairs={{0,32},{32,64},{64,96},{96,128},{128,160},{160,192},{192,224},{1,3... | collective-permute-start | bytes 98312 | tf_op jit(solution)/shard_map/ppermute | solution.py:15
  198.6 2.9 %collective-permute-start.21 = (bf16[4,1,16,256]{3,2,1,0:T(8,128)(2,1)S(1)}, bf16[4,1,16,256]{3,2,1,0:T(8,128)(2,1)S(1)}, u32[]{:S(2)}, u32[]{:S(2)}) collective-permute-start(bf16[4,1,16,256]{3,2,1,0:T(8,128)(2,1)S(1)} %get-tuple-element.20), channel_id=1, source_target_pairs={{32,0},{64,32},{96,64},{128,96},{160,128},{192,160},{224,192},{33,... | collective-permute-start | bytes 98312 | tf_op jit(solution)/shard_map/ppermute | solution.py:17
  201.6 6.5 %collective-permute-done.21 = bf16[4,1,16,256]{3,2,1,0:T(8,128)(2,1)S(1)} collective-permute-done((bf16[4,1,16,256]{3,2,1,0:T(8,128)(2,1)S(1)}, bf16[4,1,16,256]{3,2,1,0:T(8,128)(2,1)S(1)}, u32[]{:S(2)}, u32[]{:S(2)}) %collective-permute-start.21) | collective-permute-done | bytes 32800 | tf_op jit(solution)/shard_map/ppermute | solution.py:17
  208.3 3.3 %collective-permute-start.22 = (bf16[4,34,1,256]{3,2,1,0:T(2,128)(2,1)S(1)}, bf16[4,34,1,256]{3,2,1,0:T(2,128)(2,1)S(1)}, u32[]{:S(2)}, u32[]{:S(2)}) collective-permute-start(bf16[4,34,1,256]{3,2,1,0:T(2,128)(2,1)S(1)} %get-tuple-element.17), channel_id=1, source_target_pairs={{0,1},{1,2},{2,3},{3,4},{4,5},{5,6},{6,7},{7,8},{8,9},{9,10},{10,1... | collective-permute-start | bytes 208904 | tf_op jit(solution)/shard_map/ppermute | solution.py:15
  211.6 1.9 collective-permute-start.23
  213.9 6.8 %collective-permute-done.23 = bf16[4,34,1,256]{3,2,1,0:T(2,128)(2,1)S(1)} collective-permute-done((bf16[4,34,1,256]{3,2,1,0:T(2,128)(2,1)S(1)}, bf16[4,34,1,256]{3,2,1,0:T(2,128)(2,1)S(1)}, u32[]{:S(2)}, u32[]{:S(2)}) %collective-permute-start.23) | collective-permute-done | bytes 69664 | tf_op jit(solution)/shard_map/ppermute | solution.py:17
  225.1 3.1 %copy.67 = f32[4,32,2,18,256]{4,0,3,2,1:T(4,128)S(1)} copy(f32[4,32,2,18,256]{4,3,1,0,2:T(8,128)S(1)} %pad_maximum_fusion) | data formatting | bytes 9437184 | tf_op jit(solution)/shard_map/stack | solution.py:71
  228.2 2.8 %fusion.34 = (bf16[4,64,16,1,256]{4,0,2,1,3:T(4,128)(2,1)S(1)}, bf16[4,64,16,1,256]{4,0,2,1,3:T(4,128)(2,1)S(1)}) fusion(f32[4,64,18,256]{3,0,2,1:T(4,128)S(1)} %bitcast.118), kind=kLoop, calls=%fused_computation.55 | loop fusion | flops 7340032 | bytes 16777216 | tf_op jit(solution)/shard_map/stack | solution.py:71
  231.0 3.0 %pad_maximum_fusion.1 = bf16[4,64,16,2,256]{4,0,2,1,3:T(4,128)(2,1)S(1)} fusion(bf16[4,64,16,1,256]{4,0,2,1,3:T(4,128)(2,1)S(1)} %get-tuple-element.6, bf16[4,64,16,1,256]{4,0,2,1,3:T(4,128)(2,1)S(1)} %get-tuple-element.5), kind=kLoop, calls=%fused_computation.15 | loop fusion | flops 2097152 | bytes 8388608 | tf_op jit(solution)/shard_map/stack | solution.py:71
  234.0 6.4 %copy.70 = bf16[4,64,16,2,256]{4,3,2,1,0:T(2,128)(2,1)} copy(bf16[4,64,16,2,256]{4,0,2,1,3:T(4,128)(2,1)S(1)} %pad_maximum_fusion.1) | data formatting | bytes 8388608 | tf_op jit(solution)/shard_map/stack | solution.py:71
  240.4 7.2 %convert_element_type.72 = bf16[4,64,32,256]{3,2,1,0:T(8,128)(2,1)} reshape(bf16[4,64,16,2,256]{4,3,2,1,0:T(2,128)(2,1)} %copy.70) | data formatting | bytes 8388608 | tf_op jit(solution)/shard_map/convert_element_type | solution.py:90
  247.6 5.5 %add_convert_fusion = bf16[4,64,32,256]{3,2,1,0:T(8,128)(2,1)} fusion(f32[256]{0:T(256)S(1)} %copy-done.3, bf16[4,64,32,256]{3,2,1,0:T(8,128)(2,1)} %convert_element_type.72, bf16[256,256]{1,0:T(8,128)(2,1)S(1)} %copy-done), kind=kOutput, calls=%fused_computation | convolution fusion | flops 1077936128 | bytes 8520704 | tf_op jit(solution)/shard_map/dot_general | solution.py:121
  (118 shorter events, 32.7 us)
Async XLA Ops:
  0.0 247.6 %copy-start = (bf16[256,256]{1,0:T(8,128)(2,1)S(1)}, bf16[256,256]{1,0:T(8,128)(2,1)}, u32[]{:S(2)}) copy-start(bf16[256,256]{1,0:T(8,128)(2,1)} %param.20) | copy-start | bytes 393220
  0.0 38.8 %copy-start.1 = (bf16[4,16,8,256]{3,2,1,0:T(8,128)(2,1)S(1)}, bf16[4,16,8,256]{3,2,1,0:T(8,128)(2,1)}, u32[]{:S(2)}) copy-start(bf16[4,16,8,256]{3,2,1,0:T(8,128)(2,1)} %param.12) | copy-start | bytes 786436
  0.0 21.5 %copy-start.4 = (f32[4,256]{1,0:T(4,128)S(1)}, f32[4,256]{1,0:T(4,128)}, u32[]{:S(2)}) copy-start(f32[4,256]{1,0:T(4,128)} %param.15) | copy-start | bytes 12292
  0.0 22.0 %copy-start.5 = (f32[4,256]{1,0:T(4,128)S(1)}, f32[4,256]{1,0:T(4,128)}, u32[]{:S(2)}) copy-start(f32[4,256]{1,0:T(4,128)} %param.19) | copy-start | bytes 12292
  0.0 38.8 %copy-start.7 = (bf16[4,16,8,256]{3,2,1,0:T(8,128)(2,1)S(1)}, bf16[4,16,8,256]{3,2,1,0:T(8,128)(2,1)}, u32[]{:S(2)}) copy-start(bf16[4,16,8,256]{3,2,1,0:T(8,128)(2,1)} %param.11) | copy-start | bytes 786436
  1.3 20.8 %collective-permute-start = (bf16[4,2,8,256]{3,0,2,1:T(4,128)(2,1)S(1)}, bf16[4,2,8,256]{3,0,2,1:T(4,128)(2,1)S(1)}, u32[]{:S(2)}, u32[]{:S(2)}) collective-permute-start(bf16[4,2,8,256]{3,0,2,1:T(4,128)(2,1)S(1)} %get-tuple-element.39), channel_id=1, source_target_pairs={{0,32},{32,64},{64,96},{96,128},{128,160},{160,192},{192,224},{1,3... | collective-permute-start | bytes 98312 | tf_op jit(solution)/shard_map/ppermute | solution.py:15
  5.4 16.8 %collective-permute-start.1 = (bf16[4,2,8,256]{3,0,2,1:T(4,128)(2,1)S(1)}, bf16[4,2,8,256]{3,0,2,1:T(4,128)(2,1)S(1)}, u32[]{:S(2)}, u32[]{:S(2)}) collective-permute-start(bf16[4,2,8,256]{3,0,2,1:T(4,128)(2,1)S(1)} %get-tuple-element.40), channel_id=1, source_target_pairs={{32,0},{64,32},{96,64},{128,96},{160,128},{192,160},{224,192},{33,... | collective-permute-start | bytes 98312 | tf_op jit(solution)/shard_map/ppermute | solution.py:17
  12.2 18.2 %collective-permute-start.12 = (bf16[4,2,16,256]{3,1,2,0:T(2,128)(2,1)S(1)}, bf16[4,2,16,256]{3,1,2,0:T(2,128)(2,1)S(1)}, u32[]{:S(2)}, u32[]{:S(2)}) collective-permute-start(bf16[4,2,16,256]{3,1,2,0:T(2,128)(2,1)S(1)} %get-tuple-element.23), channel_id=1, source_target_pairs={{0,32},{32,64},{64,96},{96,128},{128,160},{160,192},{192,224},{1,3... | collective-permute-start | bytes 196616 | tf_op jit(solution)/shard_map/ppermute | solution.py:15
  17.2 13.2 %collective-permute-start.13 = (bf16[4,2,16,256]{3,1,2,0:T(2,128)(2,1)S(1)}, bf16[4,2,16,256]{3,1,2,0:T(2,128)(2,1)S(1)}, u32[]{:S(2)}, u32[]{:S(2)}) collective-permute-start(bf16[4,2,16,256]{3,1,2,0:T(2,128)(2,1)S(1)} %get-tuple-element.24), channel_id=1, source_target_pairs={{32,0},{64,32},{96,64},{128,96},{160,128},{192,160},{224,192},{33,... | collective-permute-start | bytes 196616 | tf_op jit(solution)/shard_map/ppermute | solution.py:17
  22.3 16.5 %collective-permute-start.2 = (bf16[4,20,2,256]{3,0,2,1:T(4,128)(2,1)S(1)}, bf16[4,20,2,256]{3,0,2,1:T(4,128)(2,1)S(1)}, u32[]{:S(2)}, u32[]{:S(2)}) collective-permute-start(bf16[4,20,2,256]{3,0,2,1:T(4,128)(2,1)S(1)} %get-tuple-element.31), channel_id=1, source_target_pairs={{0,1},{1,2},{2,3},{3,4},{4,5},{5,6},{6,7},{7,8},{8,9},{9,10},{10,1... | collective-permute-start | bytes 245768 | tf_op jit(solution)/shard_map/ppermute | solution.py:15
  28.4 10.4 %collective-permute-start.3 = (bf16[4,20,2,256]{3,0,2,1:T(4,128)(2,1)S(1)}, bf16[4,20,2,256]{3,0,2,1:T(4,128)(2,1)S(1)}, u32[]{:S(2)}, u32[]{:S(2)}) collective-permute-start(bf16[4,20,2,256]{3,0,2,1:T(4,128)(2,1)S(1)} %get-tuple-element.32), channel_id=1, source_target_pairs={{1,0},{2,1},{3,2},{4,3},{5,4},{6,5},{7,6},{8,7},{9,8},{10,9},{11,1... | collective-permute-start | bytes 245768 | tf_op jit(solution)/shard_map/ppermute | solution.py:17
  30.5 36.8 %collective-permute-start.14 = (bf16[4,36,2,256]{3,1,2,0:T(8,128)(2,1)S(1)}, bf16[4,36,2,256]{3,1,2,0:T(8,128)(2,1)S(1)}, u32[]{:S(2)}, u32[]{:S(2)}) collective-permute-start(bf16[4,36,2,256]{3,1,2,0:T(8,128)(2,1)S(1)} %get-tuple-element.15), channel_id=1, source_target_pairs={{0,1},{1,2},{2,3},{3,4},{4,5},{5,6},{6,7},{7,8},{8,9},{9,10},{10,1... | collective-permute-start | bytes 442376 | tf_op jit(solution)/shard_map/ppermute | solution.py:15
  36.9 30.4 %collective-permute-start.15 = (bf16[4,36,2,256]{3,1,2,0:T(8,128)(2,1)S(1)}, bf16[4,36,2,256]{3,1,2,0:T(8,128)(2,1)S(1)}, u32[]{:S(2)}, u32[]{:S(2)}) collective-permute-start(bf16[4,36,2,256]{3,1,2,0:T(8,128)(2,1)S(1)} %get-tuple-element.16), channel_id=1, source_target_pairs={{1,0},{2,1},{3,2},{4,3},{5,4},{6,5},{7,6},{8,7},{9,8},{10,9},{11,1... | collective-permute-start | bytes 442376 | tf_op jit(solution)/shard_map/ppermute | solution.py:17
  44.5 9.3 %collective-permute-start.4 = (bf16[4,2,8,256]{3,0,2,1:T(4,128)(2,1)S(1)}, bf16[4,2,8,256]{3,0,2,1:T(4,128)(2,1)S(1)}, u32[]{:S(2)}, u32[]{:S(2)}) collective-permute-start(bf16[4,2,8,256]{3,0,2,1:T(4,128)(2,1)S(1)} %get-tuple-element.37), channel_id=1, source_target_pairs={{0,32},{32,64},{64,96},{96,128},{128,160},{160,192},{192,224},{1,3... | collective-permute-start | bytes 98312 | tf_op jit(solution)/shard_map/ppermute | solution.py:15
  48.0 9.8 %collective-permute-start.5 = (bf16[4,2,8,256]{3,0,2,1:T(4,128)(2,1)S(1)}, bf16[4,2,8,256]{3,0,2,1:T(4,128)(2,1)S(1)}, u32[]{:S(2)}, u32[]{:S(2)}) collective-permute-start(bf16[4,2,8,256]{3,0,2,1:T(4,128)(2,1)S(1)} %get-tuple-element.38), channel_id=1, source_target_pairs={{32,0},{64,32},{96,64},{128,96},{160,128},{192,160},{224,192},{33,... | collective-permute-start | bytes 98312 | tf_op jit(solution)/shard_map/ppermute | solution.py:17
  58.0 23.0 %collective-permute-start.6 = (bf16[4,20,2,256]{3,0,2,1:T(4,128)(2,1)S(1)}, bf16[4,20,2,256]{3,0,2,1:T(4,128)(2,1)S(1)}, u32[]{:S(2)}, u32[]{:S(2)}) collective-permute-start(bf16[4,20,2,256]{3,0,2,1:T(4,128)(2,1)S(1)} %get-tuple-element.29), channel_id=1, source_target_pairs={{0,1},{1,2},{2,3},{3,4},{4,5},{5,6},{6,7},{7,8},{8,9},{9,10},{10,1... | collective-permute-start | bytes 245768 | tf_op jit(solution)/shard_map/ppermute | solution.py:15
  65.4 15.7 %collective-permute-start.7 = (bf16[4,20,2,256]{3,0,2,1:T(4,128)(2,1)S(1)}, bf16[4,20,2,256]{3,0,2,1:T(4,128)(2,1)S(1)}, u32[]{:S(2)}, u32[]{:S(2)}) collective-permute-start(bf16[4,20,2,256]{3,0,2,1:T(4,128)(2,1)S(1)} %get-tuple-element.30), channel_id=1, source_target_pairs={{1,0},{2,1},{3,2},{4,3},{5,4},{6,5},{7,6},{8,7},{9,8},{10,9},{11,1... | collective-permute-start | bytes 245768 | tf_op jit(solution)/shard_map/ppermute | solution.py:17
  70.7 1.8 copy-start.11
  81.0 0.6 copy-start.8
  81.0 0.6 copy-start.9
  86.4 36.6 %copy-start.10 = (pred[32,3]{0,1:T(4,128)(4,1)S(1)}, pred[32,3]{0,1:T(4,128)(4,1)}, u32[]{:S(2)}) copy-start(pred[32,3]{0,1:T(4,128)(4,1)} %constant.83) | copy-start | bytes 292
  86.4 10.8 %collective-permute-start.8 = (bf16[4,1,8,256]{3,0,2,1:T(4,128)(2,1)S(1)}, bf16[4,1,8,256]{3,0,2,1:T(4,128)(2,1)S(1)}, u32[]{:S(2)}, u32[]{:S(2)}) collective-permute-start(bf16[4,1,8,256]{3,0,2,1:T(4,128)(2,1)S(1)} %get-tuple-element.35), channel_id=1, source_target_pairs={{0,32},{32,64},{64,96},{96,128},{128,160},{160,192},{192,224},{1,3... | collective-permute-start | bytes 49160 | tf_op jit(solution)/shard_map/ppermute | solution.py:15
  92.2 9.3 %collective-permute-start.9 = (bf16[4,1,8,256]{3,0,2,1:T(4,128)(2,1)S(1)}, bf16[4,1,8,256]{3,0,2,1:T(4,128)(2,1)S(1)}, u32[]{:S(2)}, u32[]{:S(2)}) collective-permute-start(bf16[4,1,8,256]{3,0,2,1:T(4,128)(2,1)S(1)} %get-tuple-element.36), channel_id=1, source_target_pairs={{32,0},{64,32},{96,64},{128,96},{160,128},{192,160},{224,192},{33,... | collective-permute-start | bytes 49160 | tf_op jit(solution)/shard_map/ppermute | solution.py:17
  101.6 29.0 %collective-permute-start.10 = (bf16[4,18,1,256]{3,0,2,1:T(4,128)(2,1)S(1)}, bf16[4,18,1,256]{3,0,2,1:T(4,128)(2,1)S(1)}, u32[]{:S(2)}, u32[]{:S(2)}) collective-permute-start(bf16[4,18,1,256]{3,0,2,1:T(4,128)(2,1)S(1)} %get-tuple-element.33), channel_id=1, source_target_pairs={{0,1},{1,2},{2,3},{3,4},{4,5},{5,6},{6,7},{7,8},{8,9},{9,10},{10,1... | collective-permute-start | bytes 110600 | tf_op jit(solution)/shard_map/ppermute | solution.py:15
  109.3 21.2 %collective-permute-start.11 = (bf16[4,18,1,256]{3,0,2,1:T(4,128)(2,1)S(1)}, bf16[4,18,1,256]{3,0,2,1:T(4,128)(2,1)S(1)}, u32[]{:S(2)}, u32[]{:S(2)}) collective-permute-start(bf16[4,18,1,256]{3,0,2,1:T(4,128)(2,1)S(1)} %get-tuple-element.34), channel_id=1, source_target_pairs={{1,0},{2,1},{3,2},{4,3},{5,4},{6,5},{7,6},{8,7},{9,8},{10,9},{11,1... | collective-permute-start | bytes 110600 | tf_op jit(solution)/shard_map/ppermute | solution.py:17
  133.3 3.1 %copy-start.2 = (bf16[256,256]{1,0:T(8,128)(2,1)S(1)}, bf16[256,256]{1,0:T(8,128)(2,1)}, u32[]{:S(2)}) copy-start(bf16[256,256]{1,0:T(8,128)(2,1)} %param.16) | copy-start | bytes 393220
  133.4 3.1 %copy-start.6 = (f32[256]{0:T(256)S(1)}, f32[256]{0:T(256)}, u32[]{:S(2)}) copy-start(f32[256]{0:T(256)} %param.17) | copy-start | bytes 3076
  139.4 9.2 %collective-permute-start.16 = (bf16[4,2,16,256]{3,2,1,0:T(8,128)(2,1)S(1)}, bf16[4,2,16,256]{3,2,1,0:T(8,128)(2,1)S(1)}, u32[]{:S(2)}, u32[]{:S(2)}) collective-permute-start(bf16[4,2,16,256]{3,2,1,0:T(8,128)(2,1)S(1)} %get-tuple-element.21), channel_id=1, source_target_pairs={{0,32},{32,64},{64,96},{96,128},{128,160},{160,192},{192,224},{1,3... | collective-permute-start | bytes 196616 | tf_op jit(solution)/shard_map/ppermute | solution.py:15
  142.9 9.8 %collective-permute-start.17 = (bf16[4,2,16,256]{3,2,1,0:T(8,128)(2,1)S(1)}, bf16[4,2,16,256]{3,2,1,0:T(8,128)(2,1)S(1)}, u32[]{:S(2)}, u32[]{:S(2)}) collective-permute-start(bf16[4,2,16,256]{3,2,1,0:T(8,128)(2,1)S(1)} %get-tuple-element.22), channel_id=1, source_target_pairs={{32,0},{64,32},{96,64},{128,96},{160,128},{192,160},{224,192},{33,... | collective-permute-start | bytes 196616 | tf_op jit(solution)/shard_map/ppermute | solution.py:17
  152.9 9.9 %collective-permute-start.18 = (bf16[4,36,2,256]{3,2,1,0:T(2,128)(2,1)S(1)}, bf16[4,36,2,256]{3,2,1,0:T(2,128)(2,1)S(1)}, u32[]{:S(2)}, u32[]{:S(2)}) collective-permute-start(bf16[4,36,2,256]{3,2,1,0:T(2,128)(2,1)S(1)} %get-tuple-element.13), channel_id=1, source_target_pairs={{0,1},{1,2},{2,3},{3,4},{4,5},{5,6},{6,7},{7,8},{8,9},{9,10},{10,1... | collective-permute-start | bytes 442376 | tf_op jit(solution)/shard_map/ppermute | solution.py:15
  160.7 9.2 %collective-permute-start.19 = (bf16[4,36,2,256]{3,2,1,0:T(2,128)(2,1)S(1)}, bf16[4,36,2,256]{3,2,1,0:T(2,128)(2,1)S(1)}, u32[]{:S(2)}, u32[]{:S(2)}) collective-permute-start(bf16[4,36,2,256]{3,2,1,0:T(2,128)(2,1)S(1)} %get-tuple-element.14), channel_id=1, source_target_pairs={{1,0},{2,1},{3,2},{4,3},{5,4},{6,5},{7,6},{8,7},{9,8},{10,9},{11,1... | collective-permute-start | bytes 442376 | tf_op jit(solution)/shard_map/ppermute | solution.py:17
  171.1 4.4 %slice-start = ((s8[4718592]{0:T(1024)(128)(4,1)}), s8[4194304]{0:T(1024)(128)(4,1)S(1)}, s32[]{:S(2)}) async-start(s8[4718592]{0:T(1024)(128)(4,1)} %bitcast.140), calls=%async_computation | async-start | bytes 8388608
  173.2 2.4 slice-start.1
  173.5 2.0 copy-start.12
  192.4 9.2 %collective-permute-start.20 = (bf16[4,1,16,256]{3,2,1,0:T(8,128)(2,1)S(1)}, bf16[4,1,16,256]{3,2,1,0:T(8,128)(2,1)S(1)}, u32[]{:S(2)}, u32[]{:S(2)}) collective-permute-start(bf16[4,1,16,256]{3,2,1,0:T(8,128)(2,1)S(1)} %get-tuple-element.19), channel_id=1, source_target_pairs={{0,32},{32,64},{64,96},{96,128},{128,160},{160,192},{192,224},{1,3... | collective-permute-start | bytes 98312 | tf_op jit(solution)/shard_map/ppermute | solution.py:15
  198.6 9.5 %collective-permute-start.21 = (bf16[4,1,16,256]{3,2,1,0:T(8,128)(2,1)S(1)}, bf16[4,1,16,256]{3,2,1,0:T(8,128)(2,1)S(1)}, u32[]{:S(2)}, u32[]{:S(2)}) collective-permute-start(bf16[4,1,16,256]{3,2,1,0:T(8,128)(2,1)S(1)} %get-tuple-element.20), channel_id=1, source_target_pairs={{32,0},{64,32},{96,64},{128,96},{160,128},{192,160},{224,192},{33,... | collective-permute-start | bytes 98312 | tf_op jit(solution)/shard_map/ppermute | solution.py:17
  208.3 5.5 %collective-permute-start.22 = (bf16[4,34,1,256]{3,2,1,0:T(2,128)(2,1)S(1)}, bf16[4,34,1,256]{3,2,1,0:T(2,128)(2,1)S(1)}, u32[]{:S(2)}, u32[]{:S(2)}) collective-permute-start(bf16[4,34,1,256]{3,2,1,0:T(2,128)(2,1)S(1)} %get-tuple-element.17), channel_id=1, source_target_pairs={{0,1},{1,2},{2,3},{3,4},{4,5},{5,6},{6,7},{7,8},{8,9},{9,10},{10,1... | collective-permute-start | bytes 208904 | tf_op jit(solution)/shard_map/ppermute | solution.py:15
  211.6 9.1 %collective-permute-start.23 = (bf16[4,34,1,256]{3,2,1,0:T(2,128)(2,1)S(1)}, bf16[4,34,1,256]{3,2,1,0:T(2,128)(2,1)S(1)}, u32[]{:S(2)}, u32[]{:S(2)}) collective-permute-start(bf16[4,34,1,256]{3,2,1,0:T(2,128)(2,1)S(1)} %get-tuple-element.18), channel_id=1, source_target_pairs={{1,0},{2,1},{3,2},{4,3},{5,4},{6,5},{7,6},{8,7},{9,8},{10,9},{11,1... | collective-permute-start | bytes 208904 | tf_op jit(solution)/shard_map/ppermute | solution.py:17
  240.4 7.2 %copy-start.3 = (f32[256]{0:T(256)S(1)}, f32[256]{0:T(256)}, u32[]{:S(2)}) copy-start(f32[256]{0:T(256)} %param.21) | copy-start | bytes 3076
where the time goes:
time: 255 us; the launch traced here: 253 us
  starting transfers between devices  117 us (46%)
  matrix products  37.9 us (15%)
  local copies, waits for them, and re-layouts  36.2 us (14%)
  waiting for transfers between devices  33.3 us (13%)
  other arithmetic  27.4 us (11%)
    ppermute x12, starting transfers between devices, extended(): lax.ppermute(tail, axis, [(i, (i + 1) % count) for i in range(ends)])  66.8 us
    ppermute x12, starting transfers between devices, extended(): lax.ppermute(head, axis, [((i + 1) % count, i) for i in range(ends)])  50.4 us
    ppermute x12, waiting for transfers between devices, extended(): lax.ppermute(head, axis, [((i + 1) % count, i) for i in range(ends)])  32.8 us
    conv_general_dilated x6, matrix products, valid_conv(): lax.conv_general_dilated(padded, kernel, (1, 1), 'VALID', dimension_numbe...  29.5 us
    another operation x4, local copies, waits for them, and re-layouts, double_inner(): jnp.stack([0.75 * values + 0.25 * before, 0.75 * values + 0.25 * after],...  10.9 us
    another operation x8, other arithmetic, double_inner(): jnp.stack([0.75 * values + 0.25 * before, 0.75 * values + 0.25 * after],...  8.69 us
    convert_element_type x2, local copies, waits for them, and re-layouts, upsample_tile(): return double_inner(rowwise, 2).astype(jnp.bfloat16)  8.43 us
    conv_general_dilated x4, other arithmetic, valid_conv(): lax.conv_general_dilated(padded, kernel, (1, 1), 'VALID', dimension_numbe...  6.92 us
  transfers between devices with their start and end apart: 24, of which 8 were waited for; matrix products, arithmetic and copies ran while one was open for 12% of the time, Pallas kernels for 0%

commit v1 on v0

v1 whole, which is shorter than its diff:
```python
import functools

import jax
import jax.numpy as jnp
import numpy as np
from jax import lax
from jax.experimental import pallas as pl
from jax.experimental.pallas import tpu as pltpu
from jax.sharding import PartitionSpec as P

MESH = pl.DeviceIdType.MESH
F32 = jnp.float32
BF16 = jnp.bfloat16
C = 256
B = 4
HC, WC = 16, 8
HF, WF = 32, 16
DIRS = ((-1, 0), (1, 0), (0, -1), (0, 1), (-1, -1), (1, 1), (-1, 1), (1, -1))


class Halo:
    def __init__(self, height, width, rows, cols):
        self.h, self.w, self.mr, self.mc = height, width, rows, cols
        self.off = B * cols
        sizes = [rows * B * width] * 2 + [height * B * cols] * 2 + [rows * B * cols] * 4
        self.sizes = sizes
        self.starts = [sum(sizes[:d]) for d in range(8)]
        self.total = sum(sizes)

    def part(self, d):
        return pl.ds(self.starts[d], self.sizes[d])

    def span(self, step, edge, length, margin):
        if step == 0:
            return margin, length
        if step < 0:
            return (margin if edge else 0), margin
        return (length if edge else margin + length), margin

    def box(self, d, edge):
        r0, rn = self.span(DIRS[d][0], edge, self.h, self.mr)
        c0, cn = self.span(DIRS[d][1], edge, self.w, self.mc)
        return pl.ds(r0, rn), pl.ds(B * c0, B * cn), rn, B * cn


E1 = Halo(HC, WC, 2, 2)
E2 = Halo(HF, WF, 2, 2)
E3 = Halo(HC, WC, 4, 4)
E4 = Halo(HF, WF, 3, 4)
HALOS = (E1, E2, E3, E4)


def decoder(
    n_row,
    n_col,
    prev_hbm,
    skipc_hbm,
    skipf_hbm,
    wc_hbm,
    wf_hbm,
    bc_ref,
    bf_ref,
    proj_ref,
    offset_ref,
    permc_ref,
    permf_ref,
    upc_ref,
    out_ref,
    prev_in,
    skipc_in,
    skipf_in,
    wc,
    wf,
    s1c,
    s1f,
    s2c,
    s2f,
    pc,
    a0c,
    a4c,
    g0c,
    g4c,
    a0f,
    a4f,
    g0f,
    g4f,
    tc,
    joined,
    sb1,
    sb2,
    sb3,
    sb4,
    rb1,
    rb2,
    rb3,
    rb4,
    load_sem,
    send_sem,
    recv_sem,
):
    row = lax.axis_index("row")
    col = lax.axis_index("col")
    sends = (sb1, sb2, sb3, sb4)
    recvs = (rb1, rb2, rb3, rb4)

    def exists(d):
        dr, dc = DIRS[d]
        ok = None
        for coord, step, count in ((row, dr, n_row), (col, dc, n_col)):
            if step:
                test = (coord > 0) if step < 0 else (coord < count - 1)
                ok = test if ok is None else ok & test
        return ok

    def each(fn):
        for d in range(8):
            pl.when(exists(d))(functools.partial(fn, d))

    def peer(d):
        return (row + DIRS[d][0], col + DIRS[d][1])

    barrier = pltpu.get_barrier_semaphore()

    def greet(d):
        pl.semaphore_signal(barrier, inc=1, device_id=peer(d), device_id_type=MESH)

    each(greet)

    loads = []
    for src, dst in (
        [(skipc_hbm, skipc_in), (skipf_hbm, skipf_in), (prev_hbm, prev_in)]
        + [(wc_hbm.at[k], wc.at[k]) for k in (0, 1)]
        + [(wf_hbm.at[k], wf.at[k]) for k in (0, 1)]
        + [(wc_hbm.at[k], wc.at[k]) for k in (2, 3)]
        + [(wf_hbm.at[k], wf.at[k]) for k in (2, 3)]
    ):
        copy = pltpu.make_async_copy(src, dst, load_sem.at[len(loads)])
        copy.start()
        loads.append(copy)
    load_skipc, load_skipf, load_prev = loads[:3]
    load_c = [loads[3], loads[4], loads[7], loads[8]]
    load_f = [loads[5], loads[6], loads[9], loads[10]]

    def copy_of(e, d):
        halo = HALOS[e]
        return pltpu.make_async_remote_copy(
            src_ref=sends[e].at[halo.part(d)],
            dst_ref=recvs[e].at[halo.part(d ^ 1)],
            send_sem=send_sem.at[e, d],
            recv_sem=recv_sem.at[e, d ^ 1],
            device_id=peer(d),
            device_id_type=MESH,
        )

    def arrival_of(e, d):
        halo = HALOS[e]
        return pltpu.make_async_remote_copy(
            src_ref=sends[e].at[halo.part(d)],
            dst_ref=recvs[e].at[halo.part(d)],
            send_sem=send_sem.at[e, d],
            recv_sem=recv_sem.at[e, d],
            device_id=peer(d),
            device_id_type=MESH,
        )

    def pack(e, values):
        halo = HALOS[e]
        for d in range(8):
            rows, cols, rn, cn = halo.box(d, True)
            tile = values[rows, cols, :].reshape(rn * cn, C)
            sends[e][halo.part(d), :] = tile.astype(BF16)

    def send(e):
        each(lambda d: copy_of(e, d).start())

    def receive(e, values):
        halo = HALOS[e]

        def take(d):
            arrival_of(e, d).wait_recv()
            rows, cols, rn, cn = halo.box(d, False)
            tile = recvs[e][halo.part(d), :].astype(F32)
            values[rows, cols, :] = tile.reshape(rn, cn, C)

        each(take)

    def relayout(src, perm, height, width, dst, row0, off):
        group = 4

        def step(i, carry):
            for j in range(group):
                h = i * group + j
                flat = src[:, h].astype(F32).reshape(B * width, C).astype(BF16)
                dst[row0 + h, pl.ds(off, B * width), :] = jnp.dot(
                    perm[...], flat, preferred_element_type=F32
                )
            return carry

        lax.fori_loop(0, height // group, step, 0)

    def activate(values, shift, height, width, a0, a4, extra=None):
        n = B * width
        group = 2

        def step(i, carry):
            h = i * group
            if extra is not None:
                values[pl.ds(h, group)] = values[pl.ds(h, group)] + extra[pl.ds(h + 1, group)]
            v = jnp.maximum(values[pl.ds(h, group), pl.ds(shift, n), :], 0.0)
            a0[pl.ds(h, group), pl.ds(0, n), :] = v
            a4[pl.ds(h, group), pl.ds(B, n), :] = v
            return carry

        lax.fori_loop(0, height // group, step, 0)

    def zero_outside(a0, a4, margin, height, width):
        full = B * (width + 2 * margin)

        def wipe(r0, rn, c0, cn):
            blank = jnp.zeros((rn, cn, C), F32)
            a0[pl.ds(r0, rn), pl.ds(c0, cn), :] = blank
            a4[pl.ds(r0, rn), pl.ds(c0 + B, cn), :] = blank

        tall = height + 2 * margin
        pl.when(row == 0)(lambda: wipe(0, margin, 0, full))
        pl.when(row == n_row - 1)(lambda: wipe(margin + height, margin, 0, full))
        pl.when(col == 0)(lambda: wipe(0, tall, 0, B * margin))
        pl.when(col == n_col - 1)(lambda: wipe(0, tall, B * (margin + width), B * margin))

    def conv(a0, a4, w, k, bias, height, width, chunk, emit):
        n = B * width

        def step(i, carry):
            h = jnp.minimum(i * chunk, height - chunk)
            total = None
            for dy in range(3):
                for dx in range(3):
                    src = a4 if dx == 1 else a0
                    first = 8 if dx else 0
                    tap = src[pl.ds(h + dy, chunk), pl.ds(first, n), :]
                    part = jnp.dot(
                        tap.reshape(chunk * n, C).astype(BF16),
                        w[k, 3 * dy + dx],
                        preferred_element_type=F32,
                    )
                    total = part if total is None else total + part
            emit(h, (total + bias[pl.ds(k, 1), :]).reshape(chunk, n, C))
            return carry

        steps = -(-height // chunk)
        if steps == 1:
            step(0, 0)
        else:
            lax.fori_loop(0, steps, step, 0)

    def to_hidden(g0, g4, width, chunk):
        def emit(h, r):
            r = jnp.maximum(r, 0.0)
            g0[pl.ds(h, chunk), pl.ds(0, B * width), :] = r
            g4[pl.ds(h, chunk), pl.ds(B, B * width), :] = r

        return emit

    load_skipc.wait()
    relayout(skipc_in, permc_ref, HC, WC, s1c, E1.mr, E1.off)
    pack(0, s1c)
    load_skipf.wait()
    relayout(skipf_in, permf_ref, HF, WF, s1f, E2.mr, E2.off)
    pack(1, s1f)
    tall_peers = (row > 0).astype(jnp.int32) + (row < n_row - 1).astype(jnp.int32)
    wide_peers = (col > 0).astype(jnp.int32) + (col < n_col - 1).astype(jnp.int32)
    pl.semaphore_wait(barrier, tall_peers + wide_peers + tall_peers * wide_peers)
    send(0)
    send(1)
    load_prev.wait()
    relayout(prev_in, permc_ref, HC, WC, pc, 0, 0)

    receive(0, s1c)
    activate(s1c, 0, HC + 4, WC + 4, a0c, a4c)
    zero_outside(a0c, a4c, 2, HC, WC)
    load_c[0].wait()
    conv(a0c, a4c, wc, 0, bc_ref, HC + 2, WC + 2, HC + 2, to_hidden(g0c, g4c, WC + 2, HC + 2))
    zero_outside(g0c, g4c, 1, HC, WC)

    def emit_sum_coarse(h, r):
        own = s1c[pl.ds(E1.mr, HC), pl.ds(E1.off, B * WC), :]
        s2c[pl.ds(E3.mr, HC), pl.ds(E3.off, B * WC), :] = r + own + pc[...]

    load_c[1].wait()
    conv(g0c, g4c, wc, 1, bc_ref, HC, WC, HC, emit_sum_coarse)
    pack(2, s2c)
    send(2)

    receive(1, s1f)
    activate(s1f, 0, HF + 4, WF + 4, a0f, a4f)
    zero_outside(a0f, a4f, 2, HF, WF)
    load_f[0].wait()
    conv(a0f, a4f, wf, 0, bf_ref, HF + 2, WF + 2, 12, to_hidden(g0f, g4f, WF + 2, 12))
    zero_outside(g0f, g4f, 1, HF, WF)

    def emit_unit_fine(h, r):
        own = s1f[pl.ds(h + E2.mr, 16), pl.ds(E2.off, B * WF), :]
        s2f[pl.ds(h + E4.mr, 16), pl.ds(E4.off, B * WF), :] = r + own

    load_f[1].wait()
    conv(g0f, g4f, wf, 1, bf_ref, HF, WF, 16, emit_unit_fine)
    pack(3, s2f)
    send(3)

    receive(2, s2c)
    activate(s2c, 0, HC + 8, WC + 8, a0c, a4c)
    zero_outside(a0c, a4c, 4, HC, WC)
    load_c[2].wait()
    conv(a0c, a4c, wc, 2, bc_ref, HC + 6, WC + 6, HC + 6, to_hidden(g0c, g4c, WC + 6, HC + 6))
    zero_outside(g0c, g4c, 3, HC, WC)
    tall, wide = HC + 4, B * (WC + 4)

    def emit_top_coarse(h, r):
        tc[pl.ds(1, tall), :, :] = (r + s2c[pl.ds(2, tall), pl.ds(8, wide), :]).astype(BF16)

    load_c[3].wait()
    conv(g0c, g4c, wc, 3, bc_ref, HC + 4, WC + 4, HC + 4, emit_top_coarse)

    tc[0] = jnp.zeros((wide, C), BF16)
    tc[tall + 1] = jnp.zeros((wide, C), BF16)

    def repeat_rows(buf, dst, src):
        for r in dst:
            buf[r] = buf[src]

    def repeat_cols(buf, height, width, dst, src):
        def step(h, carry):
            v = buf[h].astype(F32)
            parts = [v[B * j : B * j + B] for j in range(width)]
            for j in dst:
                parts[j] = parts[src]
            buf[h] = jnp.concatenate(parts + [v[B * width :]] if v.shape[0] > B * width else parts, axis=0).astype(BF16)
            return carry

        lax.fori_loop(0, height, step, 0)

    pl.when(row == 0)(lambda: repeat_rows(tc, (1, 2), 3))
    pl.when(row == n_row - 1)(lambda: repeat_rows(tc, (HC + 3, HC + 4), HC + 2))
    pl.when(col == 0)(lambda: repeat_cols(tc, HC + 6, WC + 4, (0, 1), 2))
    pl.when(col == n_col - 1)(lambda: repeat_cols(tc, HC + 6, WC + 4, (WC + 2, WC + 3), WC + 1))

    def join(i, carry):
        for j in range(2):
            k = 2 * i + j
            near = tc[pl.ds(k, 3)].reshape(3 * wide, C)
            up = jnp.dot(upc_ref[...], near, preferred_element_type=F32).astype(BF16)
            r = jnp.dot(up, proj_ref[...], preferred_element_type=F32) + offset_ref[...]
            joined[pl.ds(2 * k, 2)] = r.astype(BF16).astype(F32).reshape(2, 2 * wide, C)
        return carry

    lax.fori_loop(0, tall // 2, join, 0)

    receive(3, s2f)
    activate(s2f, B, HF + 6, WF + 6, a0f, a4f, joined)
    zero_outside(a0f, a4f, 3, HF, WF)
    load_f[2].wait()
    conv(a0f, a4f, wf, 2, bf_ref, HF + 4, WF + 4, 12, to_hidden(g0f, g4f, WF + 4, 12))
    zero_outside(g0f, g4f, 2, HF, WF)
    n = B * (WF + 2)

    def emit_top_fine(h, r):
        own = s2f[pl.ds(h + 2, 12), pl.ds(3 * B, n), :]
        pad = jnp.zeros((12, 8, C), F32)
        out_ref[pl.ds(h, 12)] = jnp.concatenate([r + own, pad], axis=1).astype(BF16)

    load_f[3].wait()
    conv(g0f, g4f, wf, 3, bf_ref, HF + 2, WF + 2, 12, emit_top_fine)
    pl.when(row == 0)(lambda: repeat_rows(out_ref, (0,), 1))
    pl.when(row == n_row - 1)(lambda: repeat_rows(out_ref, (HF + 1,), HF))
    pl.when(col == 0)(lambda: repeat_cols(out_ref, HF + 2, WF + 2, (0,), 1))
    pl.when(col == n_col - 1)(lambda: repeat_cols(out_ref, HF + 2, WF + 2, (WF + 1,), WF))

    for e in range(4):
        each(lambda d, e=e: copy_of(e, d).wait_send())


def finish(top_ref, up_ref, proj_ref, offset_ref, out_ref):
    start = pl.program_id(0) * 4
    for j in range(4):
        near = top_ref[pl.ds(start + j, 3)].reshape(3 * B * (WF + 4), C)
        up = jnp.dot(up_ref[...], near, preferred_element_type=F32).astype(BF16)
        r = jnp.dot(up, proj_ref[...], preferred_element_type=F32) + offset_ref[...]
        r = r.astype(BF16).reshape(2, B, 2 * WF, C)
        out_ref[:, 2 * j] = r[0]
        out_ref[:, 2 * j + 1] = r[1]


def interleave(width):
    m = np.zeros((B * width, B * width), np.float32)
    for w in range(width):
        for b in range(B):
            m[w * B + b, b * width + w] = 1.0
    return m


def doubling(cols, out_cols, pitch, place, first):
    m = np.zeros((2 * B * out_cols, 3 * pitch), np.float32)
    for parity in range(2):
        for f in range(out_cols):
            c = first + f // 2
            beside = min(max(c + (1 if f % 2 else -1), 0), cols - 1)
            for b in range(B):
                out = parity * B * out_cols + place(f, b)
                for r, wr in ((1, 0.75), (2 if parity else 0, 0.25)):
                    m[out, r * pitch + c * B + b] += 0.75 * wr
                    m[out, r * pitch + beside * B + b] += 0.25 * wr
    return m


def per_device(n_row, n_col, previous, skip_coarse, skip_fine, coarse_convs, coarse_biases, coarse_project,
               coarse_offset, fine_convs, fine_biases, fine_project, fine_offset):
    wc = coarse_convs.reshape(4, 9, C, C)
    wf = fine_convs.reshape(4, 9, C, C)
    permc = jnp.asarray(interleave(WC), BF16)
    permf = jnp.asarray(interleave(WF), BF16)
    upc = jnp.asarray(doubling(WC + 4, 2 * (WC + 4), B * (WC + 4), lambda f, b: f * B + b, 0), BF16)
    upf = jnp.asarray(doubling(WF + 2, 2 * WF, B * (WF + 4), lambda f, b: b * 2 * WF + f, 1), BF16)
    vmem = pl.BlockSpec(memory_space=pltpu.VMEM)
    anywhere = pl.BlockSpec(memory_space=pl.ANY)

    def block(rows, subs, dtype=F32):
        return pltpu.VMEM((rows, subs, C), dtype)

    top = pl.pallas_call(
        functools.partial(decoder, n_row, n_col),
        out_shape=jax.ShapeDtypeStruct((HF + 2, B * (WF + 4), C), BF16),
        in_specs=[anywhere] * 5 + [vmem] * 7,
        out_specs=vmem,
        scratch_shapes=[
            pltpu.VMEM((B, HC, WC, C), BF16),
            pltpu.VMEM((B, HC, WC, C), BF16),
            pltpu.VMEM((B, HF, WF, C), BF16),
            pltpu.VMEM((4, 9, C, C), BF16),
            pltpu.VMEM((4, 9, C, C), BF16),
            block(HC + 4, B * (WC + 4)),
            block(HF + 4, B * (WF + 4)),
            block(HC + 8, B * (WC + 8)),
            block(HF + 6, B * (WF + 8)),
            block(HC, B * WC),
            block(HC + 8, B * (WC + 8)),
            block(HC + 8, B * (WC + 8) + 8),
            block(HC + 6, B * (WC + 6)),
            block(HC + 6, B * (WC + 6) + 8),
            block(HF + 6, B * (WF + 6)),
            block(HF + 6, B * (WF + 6) + 8),
            block(HF + 4, B * (WF + 4)),
            block(HF + 4, B * (WF + 4) + 8),
            block(HC + 6, B * (WC + 4), BF16),
            block(2 * (HC + 4), 2 * B * (WC + 4)),
        ]
        + [pltpu.VMEM((halo.total, C), BF16) for halo in HALOS] * 2
        + [
            pltpu.SemaphoreType.DMA((11,)),
            pltpu.SemaphoreType.DMA((4, 8)),
            pltpu.SemaphoreType.DMA((4, 8)),
        ],
        compiler_params=pltpu.CompilerParams(
            collective_id=0, has_side_effects=True, vmem_limit_bytes=62 * 2**20
        ),
        name="decoder",
    )(
        previous,
        skip_coarse,
        skip_fine,
        wc,
        wf,
        coarse_biases,
        fine_biases,
        coarse_project,
        coarse_offset.reshape(1, C),
        permc,
        permf,
        upc,
    )
    return pl.pallas_call(
        finish,
        grid=(HF // 4,),
        out_shape=jax.ShapeDtypeStruct((B, 2 * HF, 2 * WF, C), BF16),
        in_specs=[vmem] * 4,
        out_specs=pl.BlockSpec((B, 8, 2 * WF, C), lambda i: (0, i, 0, 0)),
        compiler_params=pltpu.CompilerParams(vmem_limit_bytes=32 * 2**20),
        name="finish",
    )(top, upf, fine_project, fine_offset.reshape(1, C))


def solution(mesh):
    tiled = P(None, "row", "col", None)
    return jax.shard_map(
        functools.partial(per_device, mesh.shape["row"], mesh.shape["col"]),
        mesh=mesh,
        in_specs=(tiled,) * 3 + (P(),) * 8,
        out_specs=tiled,
        check_vma=False,
    )
```

time: 255 us -> 74.7 us (0.29)
  the two profiles are of different devices: /device:TPU:233 before, /device:TPU:29 now
where the time goes in v1:
time: 74.7 us; the launch traced here: 74.6 us
  Pallas kernels  73.2 us (98%)
  local copies, waits for them, and re-layouts  1.35 us (2%)
    pallas_call x1, Pallas kernels, per_device(): pl.pallas_call(functools.partial(decoder, n_row, n_col), out_shape=jax.Sh...  67.3 us
    pallas_call x1, Pallas kernels, per_device(): pl.pallas_call(finish, grid=(HF // 4,), out_shape=jax.ShapeDtypeStruct((B...  5.89 us

profile of v1, /device:TPU:29, one launch (start us, length us, event | category | flops | bytes accessed | tf_op | source)
XLA Modules:
  0.0 74.6 jit_solution(10094711940732018952)
XLA Ops:
  0.0 0.0 copy-start.1
  0.0 0.0 copy-start.2
  0.0 0.0 copy-start.3
  0.0 67.3 %decoder.1.top_ref = bf16[34,80,256]{2,1,0:T(8,128)(2,1)} custom-call(bf16[4,16,8,256]{3,2,1,0:T(8,128)(2,1)} %prev_hbm.1, bf16[4,16,8,256]{3,2,1,0:T(8,128)(2,1)} %skipc_hbm.1, bf16[4,32,16,256]{3,2,1,0:T(8,128)(2,1)} %skipf_hbm.1, bf16[4,9,256,256]{3,2,1,0:T(8,128)(2,1)} %bitcast.5, bf16[4,9,256,256]{3,2,1,0:T(8,128)(2,1)} %bitcast.6, f32[4,256]{1,0:T(4,128)} %bc_ref.1, ...), custom_call_target="tpu_custom_call" | custom-call | tf_op jit(solution)/shard_map/decoder/pallas_call | solution.py:429
  67.4 0.0 copy-done.1
  67.4 0.0 copy-done.2
  67.4 0.0 copy-done.3
  67.4 0.0 copy-start
  67.4 1.3 %copy-done = bf16[34,80,256]{2,1,0:T(8,128)(2,1)S(1)} copy-done((bf16[34,80,256]{2,1,0:T(8,128)(2,1)S(1)}, bf16[34,80,256]{2,1,0:T(8,128)(2,1)}, u32[]{:S(2)}) %copy-start) | copy-done | bytes 1392664
  68.7 5.9 %finish.1 = bf16[4,64,32,256]{3,2,1,0:T(8,128)(2,1)} custom-call(bf16[34,80,256]{2,1,0:T(8,128)(2,1)S(1)} %copy-done, bf16[256,240]{1,0:T(8,128)(2,1)S(1)} %copy-done.2, bf16[256,256]{1,0:T(8,128)(2,1)S(1)} %copy-done.1, f32[1,256]{1,0:T(1,128)S(1)} %bitcast.4), custom_call_target="tpu_custom_call" | custom-call | tf_op jit(solution)/shard_map/finish/pallas_call | solution.py:480
Async XLA Ops:
  0.0 67.4 %copy-start.1 = (bf16[256,256]{1,0:T(8,128)(2,1)S(1)}, bf16[256,256]{1,0:T(8,128)(2,1)}, u32[]{:S(2)}) copy-start(bf16[256,256]{1,0:T(8,128)(2,1)} %proj_ref.3) | copy-start | bytes 393220
  0.0 67.4 %copy-start.2 = (bf16[256,240]{1,0:T(8,128)(2,1)S(1)}, bf16[256,240]{1,0:T(8,128)(2,1)}, u32[]{:S(2)}) copy-start(bf16[256,240]{1,0:T(8,128)(2,1)} %constant.11.clone.up_ref) | copy-start | bytes 368644
  0.0 67.4 %copy-start.3 = (f32[256]{0:T(256)S(1)}, f32[256]{0:T(256)}, u32[]{:S(2)}) copy-start(f32[256]{0:T(256)} %param.25) | copy-start | bytes 3076
  67.4 1.3 %copy-start = (bf16[34,80,256]{2,1,0:T(8,128)(2,1)S(1)}, bf16[34,80,256]{2,1,0:T(8,128)(2,1)}, u32[]{:S(2)}) copy-start(bf16[34,80,256]{2,1,0:T(8,128)(2,1)} %decoder.1.top_ref) | copy-start | bytes 4177924
